TPU v7x, 32 devices: a whole 2x2x4 slice. The times are simulated.
32 devices in a mesh: seq: 16 (over z, y, x), head: 2 (over core).
Axes of the slice: x: 2, y: 2, z: 4, core: 2. Of those that a mesh axis runs over, the one named last changes fastest.
Arguments:
- queries: bfloat16 [2048, 2048], P('seq', 'head'), may hold values from -6 to 6
- keys: bfloat16 [2048, 512], P('seq', 'head'), may hold values from -6 to 6
- values: bfloat16 [2048, 512], P('seq', 'head'), may hold values from -6 to 6
- tile_mask: int32 [32, 32], replicated, may hold values from 0 to 1, as said below
- out_weight: bfloat16 [2048, 4096], P('head'), may hold values from -0.5 to 0.5
Outputs:
- mixed: bfloat16 [2048, 4096], P(('seq', 'head'))
Inputs may be any that keep to these rules, and one draw needn't show every extreme that they name: tile_mask[i, j] is 1 for i == j, 0 for j > i, and 0 or 1 below the diagonal.
All inputs are finite; a program needn't handle non-finite values.
Results may differ from a plain program's by a relative error of at most 0.01.
Values may be sent and summed in bfloat16 or wider, within the bound.
No kernel may reach another device: no remote copies, remote signals or barrier semaphores. Data moves between devices by JAX's collectives and lax.ppermute only.
A program may use at most 128 MiB of HBM per device.

v0:
```python
import math
import jax
import jax.numpy as jnp
from jax import lax
from jax.sharding import PartitionSpec as P

HD = 128
TILE = 64
MASK_FLOOR = -1e30


def per_device(queries, keys, values, tile_mask, out_weight):
    row_count = queries.shape[0]
    local_groups = keys.shape[1] // HD
    group = queries.shape[1] // HD // local_groups
    scale = 1.0 / math.sqrt(HD)
    seq_place = lax.axis_index("seq")
    query_index = seq_place * row_count + jnp.arange(row_count, dtype=jnp.int32)
    query_block = queries.reshape(row_count, local_groups, group, HD)
    query_tiles = query_index[::TILE] // TILE
    mask_rows = jnp.take(tile_mask, query_tiles, axis=0)

    def block_step(state, key_part, value_part, key_start):
        width = key_part.shape[0]
        key_index = key_start + jnp.arange(width, dtype=jnp.int32)
        tile_open = jnp.repeat(jnp.take(mask_rows, key_index // TILE, axis=1) > 0, TILE, axis=0)
        allowed = tile_open & (key_index[None, :] <= query_index[:, None])
        best, total, running = state
        allowed_wide = allowed[:, None, None, :]
        scores = (
            jnp.einsum(
                "qgrd,kgd->qgrk",
                query_block,
                key_part.reshape(width, local_groups, HD),
                preferred_element_type=jnp.float32,
            )
            * scale
        )
        masked = jnp.where(allowed_wide, scores, MASK_FLOOR)
        new_best = jnp.maximum(best, jnp.max(masked, axis=-1))
        weights = jnp.where(allowed_wide, jnp.exp(masked - new_best[..., None]), 0.0)
        rescale = jnp.exp(best - new_best)
        total = total * rescale + jnp.sum(weights, axis=-1)
        product = jnp.einsum(
            "qgrk,kgd->qgrd",
            weights.astype(jnp.bfloat16),
            value_part.reshape(width, local_groups, HD),
            preferred_element_type=jnp.float32,
        )
        running = running * rescale[..., None] + product
        return (new_best, total, running)

    initial = (
        jnp.full((row_count, local_groups, group), MASK_FLOOR, jnp.float32),
        jnp.zeros((row_count, local_groups, group), jnp.float32),
        jnp.zeros((row_count, local_groups, group, HD), jnp.float32),
    )
    carry = initial
    key_piece = lax.all_gather(keys, "seq", axis=0, tiled=True)
    value_piece = lax.all_gather(values, "seq", axis=0, tiled=True)
    width = key_piece.shape[0]
    block_size = math.gcd(width, 2048)
    count = width // block_size
    key_blocks = key_piece.reshape(count, block_size, key_piece.shape[1])
    value_blocks = value_piece.reshape(count, block_size, value_piece.shape[1])
    offsets = block_size * jnp.arange(count, dtype=jnp.int32)

    def advance(state, item):
        key_part, value_part, key_start = item
        return (block_step(state, key_part, value_part, key_start), None)

    carry, unused = lax.scan(advance, carry, (key_blocks, value_blocks, offsets))
    best, total, running = carry
    attended = (
        (running / total[..., None])
        .reshape(row_count, local_groups * group * HD)
        .astype(jnp.bfloat16)
    )
    return lax.psum_scatter(
        jnp.dot(attended, out_weight, preferred_element_type=jnp.float32).astype(jnp.bfloat16),
        "head",
        scatter_dimension=0,
        tiled=True,
    )


def solution(mesh):
    placed = (P("seq", "head"), P("seq", "head"), P("seq", "head"), P(), P("head", None))
    return jax.shard_map(
        per_device, mesh=mesh, in_specs=placed, out_specs=P(("seq", "head"), None), check_vma=False
    )
```

profile of v0, /device:TPU:0, one launch (start us, length us, event | category | flops | bytes accessed | tf_op | source)
XLA Modules:
  0.0 147.7 jit_solution(15410946941550882141)
XLA Ops:
  6.5 0.0 copy-start
  6.5 0.0 all-gather.3.cloned.1.call-start
  6.5 1.6 %copy.13 = bf16[128,256]{0,1:T(8,128)(2,1)} copy(bf16[128,256]{1,0:T(8,128)(2,1)} %param.6) | data formatting | bytes 131072 | tf_op args[1]
  8.1 0.0 all-gather.3.cloned.1.call-update
  8.1 0.0 all-gather.5.cloned.1.call-start
  8.2 0.7 all-gather.5.cloned.1.call-update
  8.9 0.0 reduce-scatter.2.cloned.1.call-start
  9.0 0.1 slice.3
  9.1 0.0 copy-done
  9.1 0.6 gather_fusion
  9.7 0.1 broadcast_select_fusion
  9.8 0.1 copy.10
  9.9 5.5 %gather_fusion.1 = s32[2048,2]{1,0:T(8,128)S(1)} fusion(s32[2,32]{0,1:T(8,128)S(1)} %copy.10, s32[2048]{0:T(1024)S(1)} %broadcast_clamp_fusion), kind=kCustom, calls=%fused_computation.1 | custom fusion | bytes 40960 | tf_op jit(solution)/shard_map/while/body/eval_jaxpr/jit(_take)/gather | solution.py:26
  15.3 0.3 fusion.13
  15.7 0.4 copy.11
  16.0 0.3 fusion.12
  16.3 0.5 copy.12
  16.7 1.1 reshape.123
  17.9 46.3 %all-gather.3.cloned.1.call-done = bf16[2048,256]{0,1:T(8,128)(2,1)} async-done(((bf16[128,256]{0,1:T(8,128)(2,1)}), bf16[2048,256]{0,1:T(8,128)(2,1)}) %all-gather.3.cloned.1.call-update) | async-done | bytes 1048592 | tf_op jit(solution)/shard_map/all_gather | solution.py:59
  64.2 2.7 %fusion = (f32[128,2,4]{0,2,1:T(4,128)S(1)}, f32[2,2048,128,4]{2,1,3,0:T(8,128)S(1)}) fusion(pred[128,2048]{0,1:T(8,128)(4,1)S(1)} %copy.12, bf16[2048,2,128,1]{0,2,3,1:T(8,128)(2,1)} %bitcast.47, bf16[128,2,4,128]{3,2,1,0:T(4,128)(2,1)S(1)} %reshape.123), kind=kOutput, calls=%fused_computation.4 | convolution fusion | flops 543161344 | bytes 9965568 | tf_op jit(solution)/shard_map/while/body/eval_jaxpr/qgrd,kgd->qgrk/dot_general | solution.py:31
  66.9 0.0 copy-start.1
  66.9 3.2 %copy-done.1 = f32[2,2048,128,4]{2,1,3,0:T(8,128)} copy-done((f32[2,2048,128,4]{2,1,3,0:T(8,128)}, f32[2,2048,128,4]{2,1,3,0:T(8,128)S(1)}, u32[]{:S(2)}) %copy-start.1) | copy-done | bytes 8388632
  70.1 2.0 %fusion.1 = f32[128,2,4]{0,2,1:T(4,128)S(1)} fusion(f32[2,2048,128,4]{2,1,3,0:T(8,128)S(1)} %get-tuple-element.26, f32[128,2,4]{0,2,1:T(4,128)S(1)} %broadcast_maximum_fusion, pred[128,2048]{0,1:T(8,128)(4,1)S(1)} %copy.12), kind=kLoop, calls=%fused_computation.5 | loop fusion | flops 10484736 | bytes 8658944 | tf_op jit(solution)/shard_map/while/body/eval_jaxpr/reduce_sum | solution.py:43
  72.2 48.9 %all-gather.5.cloned.1.call-done = bf16[2048,256]{1,0:T(8,128)(2,1)} async-done(((bf16[128,256]{1,0:T(8,128)(2,1)}), bf16[2048,256]{1,0:T(8,128)(2,1)}) %all-gather.5.cloned.1.call-update) | async-done | bytes 1048592 | tf_op jit(solution)/shard_map/all_gather | solution.py:60
  121.1 1.5 %copy.16 = bf16[2048,256]{0,1:T(8,128)(2,1)S(1)} copy(bf16[2048,256]{1,0:T(8,128)(2,1)} %all-gather.5.cloned.1.call-done) | data formatting | bytes 2097152 | tf_op jit(solution)/shard_map/all_gather | solution.py:60
  122.6 5.5 %fusion.17 = bf16[128,2,4,128]{0,3,2,1:T(8,128)(2,1)S(1)} fusion(bf16[2048,2,128,1]{0,2,3,1:T(8,128)(2,1)S(1)} %bitcast.48, f32[2,2048,128,4]{2,1,3,0:T(8,128)} %copy-done.1, f32[128,2,4]{0,2,1:T(4,128)S(1)} %broadcast_maximum_fusion, pred[128,2048]{0,1:T(8,128)(4,1)S(1)} %copy.12, f32[128,2,4]{0,2,1:T(4,128)S(1)} %get-tuple-element.24, ...), kind=kOutput, calls=%fused_computation.17 | convolution fusion | flops 547749888 | bytes 9973760 | tf_op jit(solution)/shard_map/while/body/eval_jaxpr/qgrk,kgd->qgrd/dot_general | solution.py:44
  128.1 5.6 %convolution_convert_fusion = bf16[128,4096]{1,0:T(8,128)(2,1)} fusion(bf16[128,1024]{0,1:T(8,128)(2,1)S(1)} %bitcast.49, bf16[1024,4096]{1,0:T(8,128)(2,1)} %param.9), kind=kOutput, calls=%fused_computation.7 | convolution fusion | flops 1074266112 | bytes 9699328 | tf_op jit(solution)/shard_map/dot_general | solution.py:80
  133.7 0.0 reduce-scatter.2.cloned.1.call-update
  133.8 7.4 %reduce-scatter.2.cloned.1.call-done = bf16[64,4096]{1,0:T(8,128)(2,1)} async-done(((bf16[128,4096]{1,0:T(8,128)(2,1)}), bf16[64,4096]{1,0:T(8,128)(2,1)}) %reduce-scatter.2.cloned.1.call-update) | async-done | bytes 524304 | tf_op jit(solution)/shard_map/reduce_scatter | solution.py:79
  (8 shorter events, 0.1 us)
Async XLA Ops:
  6.5 2.6 %copy-start = (s32[32,32]{1,0:T(8,128)S(1)}, s32[32,32]{1,0:T(8,128)}, u32[]{:S(2)}) copy-start(s32[32,32]{1,0:T(8,128)} %param.8) | copy-start | bytes 12292
  6.5 57.6 %all-gather.3.cloned.1.call-start = ((), (), s32[]{:S(2)}) async-start(), calls=%async_computation.1 | async-start | bytes 1114112 | tf_op jit(solution)/shard_map/all_gather | solution.py:59
  8.1 112.9 %all-gather.5.cloned.1.call-start = ((), (), s32[]{:S(2)}) async-start(), calls=%async_computation.2 | async-start | bytes 1114112 | tf_op jit(solution)/shard_map/all_gather | solution.py:60
  8.9 132.2 %reduce-scatter.2.cloned.1.call-start = ((), (), s32[]{:S(2)}) async-start(), calls=%async_computation.3 | async-start | bytes 1572864 | tf_op jit(solution)/shard_map/reduce_scatter | solution.py:79
  66.9 3.2 %copy-start.1 = (f32[2,2048,128,4]{2,1,3,0:T(8,128)}, f32[2,2048,128,4]{2,1,3,0:T(8,128)S(1)}, u32[]{:S(2)}) copy-start(f32[2,2048,128,4]{2,1,3,0:T(8,128)S(1)} %get-tuple-element.26) | copy-start | bytes 25165828
Sparse Core Ops, SparseCore 0:
  10.0 54.0 all-gather.2
  66.9 54.0 all-gather.4
  133.9 7.2 reduce-scatter.1
where the time goes:
time: 148 us
  waiting for transfers between devices  103 us (70%)
  local copies, waits for them, and re-layouts  14.4 us (10%)
  matrix products  13.9 us (9%)
  between operations  13.2 us (9%)
  other arithmetic  2.75 us (2%)
    all_gather x1, waiting for transfers between devices, per_device(): value_piece = lax.all_gather(values, 'seq', axis=0, tiled=True)  48.9 us
    all_gather x1, waiting for transfers between devices, per_device(): key_piece = lax.all_gather(keys, 'seq', axis=0, tiled=True)  46.3 us
    reduce_scatter x1, waiting for transfers between devices, per_device(): lax.psum_scatter(jnp.dot(attended, out_weight, preferred_element_type=jnp...  7.38 us
    dot_general x1, matrix products, per_device(): jnp.dot(attended, out_weight, preferred_element_type=jnp.float32)  5.64 us
    dot_general x1, matrix products, block_step(): jnp.einsum('qgrk,kgd->qgrd', weights.astype(jnp.bfloat16), value_part.res...  5.52 us
    gather x1, local copies, waits for them, and re-layouts, block_step(): jnp.take(mask_rows, key_index // TILE, axis=1) > 0  5.46 us
    unnamed x5, local copies, waits for them, and re-layouts  4.8 us
  transfers between devices with their start and end apart: 3, of which 3 were waited for; matrix products, arithmetic and copies ran while one was open for 9% of the time, Pallas kernels for 0%

commit v1 on v0

--- a/solution.py
+++ b/solution.py
@@ -7,6 +7,25 @@
 HD = 128
 TILE = 64
 MASK_FLOOR = -1e30
+
+
+def _check_ratios(panel, out_dim):
+    num = lax.axis_size("seq")
+    fields = []
+    for dev in range(num):
+        fields.append((dev, (dev + 1) % num))
+
+    def _unite_windows(block_now):
+        if len(block_now) == num:
+            return block_now
+        current_value = _unite_windows([lax.ppermute(block_now[0], "seq", fields), *block_now])
+        return current_value
+
+    everything = jnp.concatenate(_unite_windows([panel]), axis=out_dim)
+    work_now = jnp.roll(
+        everything, shift=(lax.axis_index("seq") + 1) * panel.shape[out_dim], axis=out_dim
+    )
+    return work_now
 
 
 def per_device(queries, keys, values, tile_mask, out_weight):
@@ -57,7 +76,7 @@
     )
     carry = initial
     key_piece = lax.all_gather(keys, "seq", axis=0, tiled=True)
-    value_piece = lax.all_gather(values, "seq", axis=0, tiled=True)
+    value_piece = _check_ratios(values, out_dim=0)
     width = key_piece.shape[0]
     block_size = math.gcd(width, 2048)
     count = width // block_size

time: 148 us -> 153 us (1.034)
  waiting for transfers between devices: 103 us -> 115 us
  matrix products: 13.9 us -> 7.16 us
  local copies, waits for them, and re-layouts: 14.4 us -> 10.7 us
  starting transfers between devices: 0.08 us -> 3.05 us
    ppermute x0 -> x15, waiting for transfers between devices: none -> 110 us  [_unite_windows(): lax.ppermute(block_now[0], 'seq', fields)]
    all_gather x1 -> x0, waiting for transfers between devices: 48.9 us -> none  [per_device(): value_piece = lax.all_gather(values, 'seq', axis=0, tiled=True)]
    all_gather x1, waiting for transfers between devices: 46.3 us -> 0.02 us  [per_device(): key_piece = lax.all_gather(keys, 'seq', axis=0, tiled=True)]
    dot_general x1, matrix products: 5.52 us -> 2.14 us  [block_step(): jnp.einsum('qgrk,kgd->qgrd', weights.astype(jnp.bfloat16), value_part.res...]
    dot_general x1, matrix products: 5.64 us -> 2.27 us  [per_device(): jnp.dot(attended, out_weight, preferred_element_type=jnp.float32)]
    ppermute x0 -> x15, starting transfers between devices: none -> 3 us  [_unite_windows(): lax.ppermute(block_now[0], 'seq', fields)]
    unnamed x5 -> x40, local copies, waits for them, and re-layouts: 4.8 us -> 1.86 us
    reduce_scatter x1, waiting for transfers between devices: 7.38 us -> 4.66 us  [per_device(): lax.psum_scatter(jnp.dot(attended, out_weight, preferred_element_type=jnp...]
  transfers between devices with their start and end apart: 3 -> 17, of which waited for: 3 -> 16; matrix products, arithmetic and copies ran while one was open for 9% -> 7% of each run, Pallas kernels for 0% -> 0%
where the time goes in v1:
time: 153 us
  waiting for transfers between devices  115 us (75%)
  between operations  13.8 us (9%)
  local copies, waits for them, and re-layouts  10.7 us (7%)
  matrix products  7.16 us (5%)
  starting transfers between devices  3.05 us (2%)
  other arithmetic  2.74 us (2%)
    ppermute x15, waiting for transfers between devices, _unite_windows(): lax.ppermute(block_now[0], 'seq', fields)  110 us
    gather x1, local copies, waits for them, and re-layouts, block_step(): jnp.take(mask_rows, key_index // TILE, axis=1) > 0  5.46 us
    reduce_scatter x1, waiting for transfers between devices, per_device(): lax.psum_scatter(jnp.dot(attended, out_weight, preferred_element_type=jnp...  4.66 us
  transfers between devices with their start and end apart: 17, of which 16 were waited for; matrix products, arithmetic and copies ran while one was open for 7% of the time, Pallas kernels for 0%

profile of v1, /device:TPU:0, one launch (start us, length us, event | category | flops | bytes accessed | tf_op | source)
XLA Modules:
  0.0 152.5 jit_solution(5617468430861336470)
XLA Ops:
  6.5 3.0 %collective-permute-start = (bf16[128,256]{1,0:T(8,128)(2,1)}, bf16[128,256]{1,0:T(8,128)(2,1)S(1)}, u32[]{:S(2)}, u32[]{:S(2)}) collective-permute-start(bf16[128,256]{1,0:T(8,128)(2,1)} %param.7), channel_id=1, source_target_pairs={{0,2},{2,4},{4,6},{6,8},{8,10},{10,12},{12,14},{14,16},{16,18},{18... | collective-permute-start | bytes 196616 | tf_op jit(solution)/shard_map/ppermute | solution.py:21
  9.5 6.4 %collective-permute-done = bf16[128,256]{1,0:T(8,128)(2,1)S(1)} collective-permute-done((bf16[128,256]{1,0:T(8,128)(2,1)}, bf16[128,256]{1,0:T(8,128)(2,1)S(1)}, u32[]{:S(2)}, u32[]{:S(2)}) %collective-permute-start) | collective-permute-done | bytes 65568 | tf_op jit(solution)/shard_map/ppermute | solution.py:21
  16.0 7.9 %collective-permute-done.1 = bf16[128,256]{1,0:T(8,128)(2,1)S(1)} collective-permute-done((bf16[128,256]{1,0:T(8,128)(2,1)S(1)}, bf16[128,256]{1,0:T(8,128)(2,1)S(1)}, u32[]{:S(2)}, u32[]{:S(2)}) %collective-permute-start.1) | collective-permute-done | bytes 65568 | tf_op jit(solution)/shard_map/ppermute | solution.py:21
  23.8 0.0 collective-permute-start.2
  23.8 7.9 %collective-permute-done.2 = bf16[128,256]{1,0:T(8,128)(2,1)S(1)} collective-permute-done((bf16[128,256]{1,0:T(8,128)(2,1)S(1)}, bf16[128,256]{1,0:T(8,128)(2,1)S(1)}, u32[]{:S(2)}, u32[]{:S(2)}) %collective-permute-start.2) | collective-permute-done | bytes 65568 | tf_op jit(solution)/shard_map/ppermute | solution.py:21
  31.7 0.0 collective-permute-start.3
  31.7 7.9 %collective-permute-done.3 = bf16[128,256]{1,0:T(8,128)(2,1)S(1)} collective-permute-done((bf16[128,256]{1,0:T(8,128)(2,1)S(1)}, bf16[128,256]{1,0:T(8,128)(2,1)S(1)}, u32[]{:S(2)}, u32[]{:S(2)}) %collective-permute-start.3) | collective-permute-done | bytes 65568 | tf_op jit(solution)/shard_map/ppermute | solution.py:21
  39.5 0.0 collective-permute-start.4
  39.5 7.9 %collective-permute-done.4 = bf16[128,256]{1,0:T(8,128)(2,1)S(1)} collective-permute-done((bf16[128,256]{1,0:T(8,128)(2,1)S(1)}, bf16[128,256]{1,0:T(8,128)(2,1)S(1)}, u32[]{:S(2)}, u32[]{:S(2)}) %collective-permute-start.4) | collective-permute-done | bytes 65568 | tf_op jit(solution)/shard_map/ppermute | solution.py:21
  47.4 8.4 %collective-permute-done.5 = bf16[128,256]{1,0:T(8,128)(2,1)S(1)} collective-permute-done((bf16[128,256]{1,0:T(8,128)(2,1)S(1)}, bf16[128,256]{1,0:T(8,128)(2,1)S(1)}, u32[]{:S(2)}, u32[]{:S(2)}) %collective-permute-start.5) | collective-permute-done | bytes 65568 | tf_op jit(solution)/shard_map/ppermute | solution.py:21
  55.9 0.0 collective-permute-start.6
  55.9 1.6 %copy.13 = bf16[128,256]{0,1:T(8,128)(2,1)} copy(bf16[128,256]{1,0:T(8,128)(2,1)} %param.6) | data formatting | bytes 131072 | tf_op args[1]
  57.4 0.0 all-gather.2.cloned.1.call-update
  57.5 0.0 reduce-scatter.2.cloned.1.call-start
  57.5 6.2 %collective-permute-done.6 = bf16[128,256]{1,0:T(8,128)(2,1)S(1)} collective-permute-done((bf16[128,256]{1,0:T(8,128)(2,1)S(1)}, bf16[128,256]{1,0:T(8,128)(2,1)S(1)}, u32[]{:S(2)}, u32[]{:S(2)}) %collective-permute-start.6) | collective-permute-done | bytes 65568 | tf_op jit(solution)/shard_map/ppermute | solution.py:21
  63.7 0.0 collective-permute-start.7
  63.7 7.9 %collective-permute-done.7 = bf16[128,256]{1,0:T(8,128)(2,1)S(1)} collective-permute-done((bf16[128,256]{1,0:T(8,128)(2,1)S(1)}, bf16[128,256]{1,0:T(8,128)(2,1)S(1)}, u32[]{:S(2)}, u32[]{:S(2)}) %collective-permute-start.7) | collective-permute-done | bytes 65568 | tf_op jit(solution)/shard_map/ppermute | solution.py:21
  71.6 0.0 collective-permute-start.8
  71.7 7.9 %collective-permute-done.8 = bf16[128,256]{1,0:T(8,128)(2,1)S(1)} collective-permute-done((bf16[128,256]{1,0:T(8,128)(2,1)S(1)}, bf16[128,256]{1,0:T(8,128)(2,1)S(1)}, u32[]{:S(2)}, u32[]{:S(2)}) %collective-permute-start.8) | collective-permute-done | bytes 65568 | tf_op jit(solution)/shard_map/ppermute | solution.py:21
  79.5 0.1 slice.3
  79.6 7.9 %collective-permute-done.9 = bf16[128,256]{1,0:T(8,128)(2,1)S(1)} collective-permute-done((bf16[128,256]{1,0:T(8,128)(2,1)S(1)}, bf16[128,256]{1,0:T(8,128)(2,1)S(1)}, u32[]{:S(2)}, u32[]{:S(2)}) %collective-permute-start.9) | collective-permute-done | bytes 65568 | tf_op jit(solution)/shard_map/ppermute | solution.py:21
  87.6 7.8 %collective-permute-done.10 = bf16[128,256]{1,0:T(8,128)(2,1)S(1)} collective-permute-done((bf16[128,256]{1,0:T(8,128)(2,1)S(1)}, bf16[128,256]{1,0:T(8,128)(2,1)S(1)}, u32[]{:S(2)}, u32[]{:S(2)}) %collective-permute-start.10) | collective-permute-done | bytes 65568 | tf_op jit(solution)/shard_map/ppermute | solution.py:21
  95.4 0.6 gather_fusion
  96.0 9.0 %collective-permute-done.11 = bf16[128,256]{1,0:T(8,128)(2,1)S(1)} collective-permute-done((bf16[128,256]{1,0:T(8,128)(2,1)S(1)}, bf16[128,256]{1,0:T(8,128)(2,1)S(1)}, u32[]{:S(2)}, u32[]{:S(2)}) %collective-permute-start.11) | collective-permute-done | bytes 65568 | tf_op jit(solution)/shard_map/ppermute | solution.py:21
  105.0 0.1 broadcast_select_fusion
  105.1 0.1 copy.10
  105.2 5.5 %gather_fusion.1 = s32[2048,2]{1,0:T(8,128)S(1)} fusion(s32[2,32]{0,1:T(8,128)S(1)} %copy.10, s32[2048]{0:T(1024)S(1)} %broadcast_clamp_fusion), kind=kCustom, calls=%fused_computation.1 | custom fusion | bytes 40960 | tf_op jit(solution)/shard_map/while/body/eval_jaxpr/jit(_take)/gather | solution.py:45
  110.6 4.1 %collective-permute-done.12 = bf16[128,256]{1,0:T(8,128)(2,1)S(1)} collective-permute-done((bf16[128,256]{1,0:T(8,128)(2,1)S(1)}, bf16[128,256]{1,0:T(8,128)(2,1)S(1)}, u32[]{:S(2)}, u32[]{:S(2)}) %collective-permute-start.12) | collective-permute-done | bytes 65568 | tf_op jit(solution)/shard_map/ppermute | solution.py:21
  114.7 7.9 %collective-permute-done.13 = bf16[128,256]{1,0:T(8,128)(2,1)S(1)} collective-permute-done((bf16[128,256]{1,0:T(8,128)(2,1)S(1)}, bf16[128,256]{1,0:T(8,128)(2,1)S(1)}, u32[]{:S(2)}, u32[]{:S(2)}) %collective-permute-start.13) | collective-permute-done | bytes 65568 | tf_op jit(solution)/shard_map/ppermute | solution.py:21
  122.6 0.3 fusion.13
  122.9 0.0 copy-start.1
  123.0 1.1 reshape.123
  124.1 0.4 copy.11
  124.5 0.3 fusion.12
  124.7 0.5 copy.12
  125.2 5.3 %collective-permute-done.14 = bf16[128,256]{1,0:T(8,128)(2,1)S(1)} collective-permute-done((bf16[128,256]{1,0:T(8,128)(2,1)S(1)}, bf16[128,256]{1,0:T(8,128)(2,1)S(1)}, u32[]{:S(2)}, u32[]{:S(2)}) %collective-permute-start.14) | collective-permute-done | bytes 65568 | tf_op jit(solution)/shard_map/ppermute | solution.py:21
  130.9 0.1 constant_dynamic-slice_fusion
  131.0 0.6 copy.16
  131.7 0.0 all-gather.2.cloned.1.call-done
  131.7 2.7 %fusion = (f32[128,2,4]{0,2,1:T(4,128)S(1)}, f32[2,2048,128,4]{2,1,3,0:T(8,128)S(1)}) fusion(pred[128,2048]{0,1:T(8,128)(4,1)S(1)} %copy.12, bf16[2048,2,128,1]{0,2,3,1:T(8,128)(2,1)} %bitcast.49, bf16[128,2,4,128]{3,2,1,0:T(4,128)(2,1)S(1)} %reshape.123), kind=kOutput, calls=%fused_computation.4 | convolution fusion | flops 543161344 | bytes 9965568 | tf_op jit(solution)/shard_map/while/body/eval_jaxpr/qgrd,kgd->qgrk/dot_general | solution.py:50
  134.4 0.0 slice-start
  134.5 2.0 %fusion.1 = f32[128,2,4]{0,2,1:T(4,128)S(1)} fusion(f32[2,2048,128,4]{2,1,3,0:T(8,128)S(1)} %get-tuple-element.26, f32[128,2,4]{0,2,1:T(4,128)S(1)} %broadcast_maximum_fusion, pred[128,2048]{0,1:T(8,128)(4,1)S(1)} %copy.12), kind=kLoop, calls=%fused_computation.5 | loop fusion | flops 10484736 | bytes 8658944 | tf_op jit(solution)/shard_map/while/body/eval_jaxpr/reduce_sum | solution.py:62
  136.5 0.0 slice-start.1
  136.5 2.1 %fusion.17 = bf16[128,2,4,128]{0,3,2,1:T(8,128)(2,1)S(1)} fusion(bf16[2048,2,128,1]{0,2,3,1:T(8,128)(2,1)S(1)} %bitcast.50, f32[2,2048,128,4]{2,1,3,0:T(8,128)S(1)} %get-tuple-element.26, f32[128,2,4]{0,2,1:T(4,128)S(1)} %broadcast_maximum_fusion, pred[128,2048]{0,1:T(8,128)(4,1)S(1)} %copy.12, f32[128,2,4]{0,2,1:T(4,128)S(1)} %get-tuple-element.24, ...), kind=kOutput, calls=%fused_computation.17 | convolution fusion | flops 547749888 | bytes 9973760 | tf_op jit(solution)/shard_map/while/body/eval_jaxpr/qgrk,kgd->qgrd/dot_general | solution.py:63
  138.7 0.1 slice-done.1
  138.7 2.3 %convolution_convert_fusion = bf16[128,4096]{1,0:T(8,128)(2,1)} fusion(bf16[128,1024]{0,1:T(8,128)(2,1)S(1)} %bitcast.51, bf16[1024,4096]{1,0:T(8,128)(2,1)S(1)} %bitcast.48), kind=kOutput, calls=%fused_computation.7 | convolution fusion | flops 1074266112 | bytes 9699328 | tf_op jit(solution)/shard_map/dot_general | solution.py:99
  141.0 0.0 reduce-scatter.2.cloned.1.call-update
  141.0 4.7 %reduce-scatter.2.cloned.1.call-done = bf16[64,4096]{1,0:T(8,128)(2,1)} async-done(((bf16[128,4096]{1,0:T(8,128)(2,1)}), bf16[64,4096]{1,0:T(8,128)(2,1)}) %reduce-scatter.2.cloned.1.call-update) | async-done | bytes 524304 | tf_op jit(solution)/shard_map/reduce_scatter | solution.py:98
  (54 shorter events, 0.3 us)
Async XLA Ops:
  6.5 88.9 %copy-start = (s32[32,32]{1,0:T(8,128)S(1)}, s32[32,32]{1,0:T(8,128)}, u32[]{:S(2)}) copy-start(s32[32,32]{1,0:T(8,128)} %param.8) | copy-start | bytes 12292
  6.5 125.1 %all-gather.2.cloned.1.call-start = ((), (), s32[]{:S(2)}) async-start(), calls=%async_computation.1 | async-start | bytes 1114112 | tf_op jit(solution)/shard_map/all_gather | solution.py:78
  6.5 9.4 %collective-permute-start = (bf16[128,256]{1,0:T(8,128)(2,1)}, bf16[128,256]{1,0:T(8,128)(2,1)S(1)}, u32[]{:S(2)}, u32[]{:S(2)}) collective-permute-start(bf16[128,256]{1,0:T(8,128)(2,1)} %param.7), channel_id=1, source_target_pairs={{0,2},{2,4},{4,6},{6,8},{8,10},{10,12},{12,14},{14,16},{16,18},{18... | collective-permute-start | bytes 196616 | tf_op jit(solution)/shard_map/ppermute | solution.py:21
  16.0 7.9 %collective-permute-start.1 = (bf16[128,256]{1,0:T(8,128)(2,1)S(1)}, bf16[128,256]{1,0:T(8,128)(2,1)S(1)}, u32[]{:S(2)}, u32[]{:S(2)}) collective-permute-start(bf16[128,256]{1,0:T(8,128)(2,1)S(1)} %collective-permute-done), channel_id=1, source_target_pairs={{0,2},{2,4},{4,6},{6,8},{8,10},{10,12},{12,14},{14,16},{16,18},{18... | collective-permute-start | bytes 196616 | tf_op jit(solution)/shard_map/ppermute | solution.py:21
  23.8 7.9 %collective-permute-start.2 = (bf16[128,256]{1,0:T(8,128)(2,1)S(1)}, bf16[128,256]{1,0:T(8,128)(2,1)S(1)}, u32[]{:S(2)}, u32[]{:S(2)}) collective-permute-start(bf16[128,256]{1,0:T(8,128)(2,1)S(1)} %collective-permute-done.1), channel_id=1, source_target_pairs={{0,2},{2,4},{4,6},{6,8},{8,10},{10,12},{12,14},{14,16},{16,18},{18... | collective-permute-start | bytes 196616 | tf_op jit(solution)/shard_map/ppermute | solution.py:21
  31.7 7.9 %collective-permute-start.3 = (bf16[128,256]{1,0:T(8,128)(2,1)S(1)}, bf16[128,256]{1,0:T(8,128)(2,1)S(1)}, u32[]{:S(2)}, u32[]{:S(2)}) collective-permute-start(bf16[128,256]{1,0:T(8,128)(2,1)S(1)} %collective-permute-done.2), channel_id=1, source_target_pairs={{0,2},{2,4},{4,6},{6,8},{8,10},{10,12},{12,14},{14,16},{16,18},{18... | collective-permute-start | bytes 196616 | tf_op jit(solution)/shard_map/ppermute | solution.py:21
  39.5 7.9 %collective-permute-start.4 = (bf16[128,256]{1,0:T(8,128)(2,1)S(1)}, bf16[128,256]{1,0:T(8,128)(2,1)S(1)}, u32[]{:S(2)}, u32[]{:S(2)}) collective-permute-start(bf16[128,256]{1,0:T(8,128)(2,1)S(1)} %collective-permute-done.3), channel_id=1, source_target_pairs={{0,2},{2,4},{4,6},{6,8},{8,10},{10,12},{12,14},{14,16},{16,18},{18... | collective-permute-start | bytes 196616 | tf_op jit(solution)/shard_map/ppermute | solution.py:21
  47.4 8.4 %collective-permute-start.5 = (bf16[128,256]{1,0:T(8,128)(2,1)S(1)}, bf16[128,256]{1,0:T(8,128)(2,1)S(1)}, u32[]{:S(2)}, u32[]{:S(2)}) collective-permute-start(bf16[128,256]{1,0:T(8,128)(2,1)S(1)} %collective-permute-done.4), channel_id=1, source_target_pairs={{0,2},{2,4},{4,6},{6,8},{8,10},{10,12},{12,14},{14,16},{16,18},{18... | collective-permute-start | bytes 196616 | tf_op jit(solution)/shard_map/ppermute | solution.py:21
  55.9 7.9 %collective-permute-start.6 = (bf16[128,256]{1,0:T(8,128)(2,1)S(1)}, bf16[128,256]{1,0:T(8,128)(2,1)S(1)}, u32[]{:S(2)}, u32[]{:S(2)}) collective-permute-start(bf16[128,256]{1,0:T(8,128)(2,1)S(1)} %collective-permute-done.5), channel_id=1, source_target_pairs={{0,2},{2,4},{4,6},{6,8},{8,10},{10,12},{12,14},{14,16},{16,18},{18... | collective-permute-start | bytes 196616 | tf_op jit(solution)/shard_map/ppermute | solution.py:21
  57.5 88.2 %reduce-scatter.2.cloned.1.call-start = ((), (), s32[]{:S(2)}) async-start(), calls=%async_computation.2 | async-start | bytes 1572864 | tf_op jit(solution)/shard_map/reduce_scatter | solution.py:98
  63.7 7.9 %collective-permute-start.7 = (bf16[128,256]{1,0:T(8,128)(2,1)S(1)}, bf16[128,256]{1,0:T(8,128)(2,1)S(1)}, u32[]{:S(2)}, u32[]{:S(2)}) collective-permute-start(bf16[128,256]{1,0:T(8,128)(2,1)S(1)} %collective-permute-done.6), channel_id=1, source_target_pairs={{0,2},{2,4},{4,6},{6,8},{8,10},{10,12},{12,14},{14,16},{16,18},{18... | collective-permute-start | bytes 196616 | tf_op jit(solution)/shard_map/ppermute | solution.py:21
  71.6 7.9 %collective-permute-start.8 = (bf16[128,256]{1,0:T(8,128)(2,1)S(1)}, bf16[128,256]{1,0:T(8,128)(2,1)S(1)}, u32[]{:S(2)}, u32[]{:S(2)}) collective-permute-start(bf16[128,256]{1,0:T(8,128)(2,1)S(1)} %collective-permute-done.7), channel_id=1, source_target_pairs={{0,2},{2,4},{4,6},{6,8},{8,10},{10,12},{12,14},{14,16},{16,18},{18... | collective-permute-start | bytes 196616 | tf_op jit(solution)/shard_map/ppermute | solution.py:21
  79.5 8.0 %collective-permute-start.9 = (bf16[128,256]{1,0:T(8,128)(2,1)S(1)}, bf16[128,256]{1,0:T(8,128)(2,1)S(1)}, u32[]{:S(2)}, u32[]{:S(2)}) collective-permute-start(bf16[128,256]{1,0:T(8,128)(2,1)S(1)} %collective-permute-done.8), channel_id=1, source_target_pairs={{0,2},{2,4},{4,6},{6,8},{8,10},{10,12},{12,14},{14,16},{16,18},{18... | collective-permute-start | bytes 196616 | tf_op jit(solution)/shard_map/ppermute | solution.py:21
  87.5 7.9 %collective-permute-start.10 = (bf16[128,256]{1,0:T(8,128)(2,1)S(1)}, bf16[128,256]{1,0:T(8,128)(2,1)S(1)}, u32[]{:S(2)}, u32[]{:S(2)}) collective-permute-start(bf16[128,256]{1,0:T(8,128)(2,1)S(1)} %collective-permute-done.9), channel_id=1, source_target_pairs={{0,2},{2,4},{4,6},{6,8},{8,10},{10,12},{12,14},{14,16},{16,18},{18... | collective-permute-start | bytes 196616 | tf_op jit(solution)/shard_map/ppermute | solution.py:21
  95.4 9.6 %collective-permute-start.11 = (bf16[128,256]{1,0:T(8,128)(2,1)S(1)}, bf16[128,256]{1,0:T(8,128)(2,1)S(1)}, u32[]{:S(2)}, u32[]{:S(2)}) collective-permute-start(bf16[128,256]{1,0:T(8,128)(2,1)S(1)} %collective-permute-done.10), channel_id=1, source_target_pairs={{0,2},{2,4},{4,6},{6,8},{8,10},{10,12},{12,14},{14,16},{16,18},{18... | collective-permute-start | bytes 196616 | tf_op jit(solution)/shard_map/ppermute | solution.py:21
  105.0 9.7 %collective-permute-start.12 = (bf16[128,256]{1,0:T(8,128)(2,1)S(1)}, bf16[128,256]{1,0:T(8,128)(2,1)S(1)}, u32[]{:S(2)}, u32[]{:S(2)}) collective-permute-start(bf16[128,256]{1,0:T(8,128)(2,1)S(1)} %collective-permute-done.11), channel_id=1, source_target_pairs={{0,2},{2,4},{4,6},{6,8},{8,10},{10,12},{12,14},{14,16},{16,18},{18... | collective-permute-start | bytes 196616 | tf_op jit(solution)/shard_map/ppermute | solution.py:21
  114.7 7.9 %collective-permute-start.13 = (bf16[128,256]{1,0:T(8,128)(2,1)S(1)}, bf16[128,256]{1,0:T(8,128)(2,1)S(1)}, u32[]{:S(2)}, u32[]{:S(2)}) collective-permute-start(bf16[128,256]{1,0:T(8,128)(2,1)S(1)} %collective-permute-done.12), channel_id=1, source_target_pairs={{0,2},{2,4},{4,6},{6,8},{8,10},{10,12},{12,14},{14,16},{16,18},{18... | collective-permute-start | bytes 196616 | tf_op jit(solution)/shard_map/ppermute | solution.py:21
  122.6 7.9 %collective-permute-start.14 = (bf16[128,256]{1,0:T(8,128)(2,1)S(1)}, bf16[128,256]{1,0:T(8,128)(2,1)S(1)}, u32[]{:S(2)}, u32[]{:S(2)}) collective-permute-start(bf16[128,256]{1,0:T(8,128)(2,1)S(1)} %collective-permute-done.13), channel_id=1, source_target_pairs={{0,2},{2,4},{4,6},{6,8},{8,10},{10,12},{12,14},{14,16},{16,18},{18... | collective-permute-start | bytes 196616 | tf_op jit(solution)/shard_map/ppermute | solution.py:21
  122.9 7.7 %copy-start.1 = (bf16[128,256]{1,0:T(8,128)(2,1)S(1)}, bf16[128,256]{1,0:T(8,128)(2,1)}, u32[]{:S(2)}) copy-start(bf16[128,256]{1,0:T(8,128)(2,1)} %param.7) | copy-start | bytes 196612
  134.4 4.2 %slice-start = ((s8[8388608]{0:T(1024)(128)(4,1)}), s8[4194304]{0:T(1024)(128)(4,1)S(1)}, s32[]{:S(2)}) async-start(s8[8388608]{0:T(1024)(128)(4,1)} %bitcast.47), calls=%async_computation.3 | async-start | bytes 8388608
  136.5 2.2 %slice-start.1 = ((s8[8388608]{0:T(1024)(128)(4,1)}), s8[4194304]{0:T(1024)(128)(4,1)S(1)}, s32[]{:S(2)}) async-start(s8[8388608]{0:T(1024)(128)(4,1)} %bitcast.47), calls=%async_computation.4 | async-start | bytes 8388608
Sparse Core Ops, SparseCore 0:
  57.6 54.3 all-gather.1
  141.1 4.4 reduce-scatter.1
